TPU v7x, 256 devices: a whole 4x4x8 slice. The times are simulated.
256 devices in a mesh: grp: 2 (over core), seq: 16 (over z, x_lo), head: 8 (over x_hi, y).
Axes of the slice: x: 4 (x_hi: 2, x_lo: 2; x = x_hi * 2 + x_lo), y: 4, z: 8, core: 2. Of those that a mesh axis runs over, the one named last changes fastest.
Arguments:
- patches: bfloat16 [4096, 1152], P(('grp', 'seq'), 'head'), may hold values from -200 to 200
- frames: int32 [4096], replicated, may hold values from 0 to 63, never falling along the last dimension, each value on 1 to 128 neighbouring positions
- enc_qkv: bfloat16 [3, 1152, 1152], P(None, None, 'head'), may hold values from -0.1875 to 0.1875
- enc_out: bfloat16 [1152, 1152], P('head'), may hold values from -0.1875 to 0.1875
- merge_gain: float32 [2, 4608], replicated, may hold values from 0.5 to 1.5
- merge_w: bfloat16 [2, 4608, 5120], P(None, ('grp', 'seq'), 'head'), may hold values from -0.09375 to 0.09375
- embedded: bfloat16 [8192, 5120], P(('grp', 'seq'), 'head'), may hold values from -200 to 200
- source: int32 [8192], P(('grp', 'seq')), may hold values from -1 to 1023, as said below
- dec_q: bfloat16 [5120, 4096], P(('grp', 'seq'), 'head'), may hold values from -0.078125 to 0.078125
- dec_kv: bfloat16 [5120, 2048], P(('grp', 'seq'), 'head'), may hold values from -0.078125 to 0.078125
- cotangent: bfloat16 [8192, 2, 5120], P(('grp', 'seq'), None, 'head'), may hold values from -6 to 6
Outputs:
- merged: bfloat16 [2, 1024, 5120], P(None, ('grp', 'seq'), 'head')
- context: bfloat16 [8192, 4096], P(('grp', 'seq'), 'head')
- level_grads: float32 [2, 1024, 5120], P(None, ('grp', 'seq'), 'head')
Inputs may be any that keep to these rules, and one draw needn't show every extreme that they name: `frames`: frame numbers never fall along the patches and no frame holds more than 128 patches. `source`: every merged token 0 to 1023 stands at exactly one position; all other positions hold -1; the rows of one device hold exactly 32 merged tokens, and at most 4 of those in one aligned block of 32 merged tokens, a most that some device reaches in every draw.
All inputs are finite; a program needn't handle non-finite values.
Results may differ from a plain program's by a relative error of at most 0.03.
The roundings to bfloat16 on the way count: a program that leaves them out, or rounds other values in their place, can miss the bound.
Values may be sent and summed in bfloat16 or wider, within the bound.
No kernel may reach another device: no remote copies, remote signals or barrier semaphores. Data moves between devices by JAX's collectives and lax.ppermute only.
A program may use at most 128 MiB of HBM per device.

v0:
```python
import jax
import jax.numpy as jnp
from jax import lax
from jax.sharding import PartitionSpec as P

ENC_HEADS = 16
HEAD_DIM = 128
RETURN_MOST = 4


def in_order(tiles, dim):
    shape = list(tiles.shape[1:])
    shape[dim] *= tiles.shape[0]
    return jnp.moveaxis(tiles, 0, dim).reshape(shape)


def from_everyone(value, axis):
    length = lax.axis_size(axis)
    return lax.all_to_all(
        jnp.broadcast_to(value[None], (length, *value.shape)), axis, 0, 0, tiled=True
    )


def gather_directly(value, axis, dim):
    return in_order(from_everyone(value, axis), dim)


def extended(value, sides, width):
    edges = {}
    for axis, dim in sides:
        size, length = (lax.axis_size(axis), value.shape[dim])
        up = [(i, (i + 1) % size) for i in range(size - 1)]
        last = lax.slice_in_dim(value, length - width, length, axis=dim)
        first = lax.slice_in_dim(value, 0, width, axis=dim)
        edges[dim] = (
            lax.ppermute(last, axis, up),
            lax.ppermute(first, axis, [(b, a) for a, b in up]),
        )
    done = []
    for _, dim in sides:
        low, high = edges[dim]
        around = [(width, width) if d in done else (0, 0) for d in range(value.ndim)]
        value = jnp.concatenate([jnp.pad(low, around), value, jnp.pad(high, around)], axis=dim)
        done.append(dim)
    return value


def in_blocks(value, dim, length):
    before, after = (value.shape[:dim], value.shape[dim + 1 :])
    return jnp.moveaxis(value.reshape(*before, length, -1, *after), dim, 0)


def summed_on_arrival(value, axis, dim):
    tiles = in_blocks(value, dim, lax.axis_size(axis))
    arrived = lax.all_to_all(tiles, axis, split_axis=0, concat_axis=0, tiled=True)
    return arrived.astype(jnp.float32).sum(axis=0)


def in_one_piece(arrays, axis, dim, along):
    ends, at = ([], 0)
    for a in arrays[:-1]:
        at += a.shape[along]
        ends.append(at)
    both = jnp.concatenate(arrays, axis=along)
    return tuple(jnp.split(lax.all_gather(both, axis, axis=dim, tiled=True), ends, axis=along))


def rms_rows(rows, gain):
    wide = rows.astype(jnp.float32)
    mean_sq = jnp.mean(wide * wide, axis=-1, keepdims=True)
    return wide * lax.rsqrt(mean_sq + 1e-06) * gain


def shards(
    patches,
    frames,
    enc_qkv,
    enc_out,
    merge_gain,
    merge_w,
    embedded,
    source,
    dec_q,
    dec_kv,
    cotangent,
):
    place = lax.axis_index(("grp", "seq"))
    pat_rows = patches.shape[0]
    full_patches = gather_directly(patches, "head", 1)
    enc_width = full_patches.shape[1]
    local_cols = enc_qkv.shape[2]
    enc_dim = enc_width // ENC_HEADS
    local_heads = local_cols // enc_dim
    enc_q = jnp.dot(full_patches, enc_qkv[0], preferred_element_type=jnp.float32).astype(
        jnp.bfloat16
    )
    enc_k = jnp.dot(full_patches, enc_qkv[1], preferred_element_type=jnp.float32).astype(
        jnp.bfloat16
    )
    enc_v = jnp.dot(full_patches, enc_qkv[2], preferred_element_type=jnp.float32).astype(
        jnp.bfloat16
    )
    paired = jnp.concatenate([enc_k, enc_v], axis=1)
    widened = extended(paired, ((("grp", "seq"), 0),), pat_rows)
    padded_frames = jnp.pad(frames, (pat_rows, pat_rows), constant_values=-1)
    key_frames = lax.dynamic_slice_in_dim(padded_frames, place * pat_rows, 3 * pat_rows)
    own_frames = lax.dynamic_slice_in_dim(frames, place * pat_rows, pat_rows)
    same = own_frames[:, None] == key_frames[None, :]
    query3 = enc_q.reshape(pat_rows, local_heads, enc_dim)
    keys3 = widened[:, :local_cols].reshape(3 * pat_rows, local_heads, enc_dim)
    values3 = widened[:, local_cols:].reshape(3 * pat_rows, local_heads, enc_dim)
    scores = jnp.einsum(
        "qhd,khd->hqk", query3, keys3, preferred_element_type=jnp.float32
    ) / jnp.sqrt(jnp.float32(enc_dim))
    scores = jnp.where(same[None], scores, jnp.float32(-1e30))
    top = jnp.max(scores, axis=2, keepdims=True)
    weights = jnp.where(same[None], jnp.exp(scores - top), jnp.float32(0.0))
    total = jnp.sum(weights, axis=2)
    mixed = jnp.einsum(
        "hqk,khd->qhd", weights.astype(jnp.bfloat16), values3, preferred_element_type=jnp.float32
    )
    enc_attn = (
        (mixed / jnp.transpose(total)[:, :, None])
        .astype(jnp.bfloat16)
        .reshape(pat_rows, local_cols)
    )
    partial_out = jnp.dot(enc_attn, enc_out, preferred_element_type=jnp.float32)
    summed = summed_on_arrival(partial_out.astype(jnp.bfloat16), "head", 1)
    enc_hidden = (patches.astype(jnp.float32) + summed).astype(jnp.bfloat16)
    full_hidden = gather_directly(enc_hidden, "head", 1)
    merged_rows = pat_rows // 4
    stacked = jnp.stack(
        [
            full_patches.reshape(merged_rows, 4 * enc_width),
            full_hidden.reshape(merged_rows, 4 * enc_width),
        ]
    )
    normed = rms_rows(stacked, merge_gain[:, None, :]).astype(jnp.bfloat16)
    block = normed
    merged = jnp.einsum(
        "lrk,lkc->lrc",
        block,
        lax.all_gather(merge_w, ("grp", "seq"), axis=1, tiled=True),
        preferred_element_type=jnp.float32,
    ).astype(jnp.bfloat16)
    tok_rows = embedded.shape[0]
    piece = lax.all_gather(merged[0], ("grp", "seq"), axis=0, tiled=True)
    picker = (source[:, None] == jnp.arange(piece.shape[0], dtype=jnp.int32)[None, :]).astype(
        jnp.bfloat16
    )
    inject = jnp.dot(picker, piece, preferred_element_type=jnp.float32)
    states = (embedded.astype(jnp.float32) + inject).astype(jnp.bfloat16)
    full_states = gather_directly(states, "head", 1)
    query_cols = dec_q.shape[1]
    pair_cols = dec_kv.shape[1]
    pieces = in_one_piece((dec_q, dec_kv), ("grp", "seq"), 0, 1)
    block = full_states
    query_sum = jnp.dot(block, pieces[0], preferred_element_type=jnp.float32)
    pair_sum = jnp.dot(block, pieces[1], preferred_element_type=jnp.float32)
    queries = query_sum.astype(jnp.bfloat16)
    keys_values = pair_sum.astype(jnp.bfloat16)
    kv_local = pair_cols // (2 * HEAD_DIM)
    group = query_cols // HEAD_DIM // kv_local
    query4 = queries.reshape(tok_rows, kv_local, group, HEAD_DIM)
    query_pos = place * tok_rows + jnp.arange(tok_rows, dtype=jnp.int32)
    scale = 1.0 / jnp.sqrt(jnp.float32(HEAD_DIM))
    piece = lax.all_gather(keys_values, ("grp", "seq"), axis=0, tiled=True)
    running_max = jnp.full((kv_local, group, tok_rows), -1e30, jnp.float32)
    count = piece.shape[0]
    split = piece.reshape(count, kv_local, 2, HEAD_DIM)
    keys = split[:, :, 0, :]
    values = split[:, :, 1, :]
    logits = jnp.einsum("qhgd,khd->hgqk", query4, keys, preferred_element_type=jnp.float32) * scale
    key_pos = jnp.arange(count, dtype=jnp.int32)
    visible = (query_pos[:, None] >= key_pos[None, :])[None, None]
    logits = jnp.where(visible, logits, jnp.float32(-1e30))
    new_max = jnp.maximum(running_max, jnp.max(logits, axis=3))
    probs = jnp.where(visible, jnp.exp(logits - new_max[..., None]), jnp.float32(0.0))
    new_sum = jnp.sum(probs, axis=3)
    new_accum = jnp.einsum(
        "hgqk,khd->hgqd", probs.astype(jnp.bfloat16), values, preferred_element_type=jnp.float32
    )
    normalized = (new_accum / new_sum[..., None]).astype(jnp.bfloat16)
    context = jnp.transpose(normalized, (2, 0, 1, 3)).reshape(tok_rows, query_cols)
    cot_flat = cotangent.reshape(tok_rows, 2 * cotangent.shape[2])
    holders = lax.axis_size(("grp", "seq"))
    capacity = RETURN_MOST
    visual = source >= 0
    holder = jnp.where(visual, source // merged_rows, -1)
    row_ids = jnp.arange(tok_rows, dtype=jnp.int32)
    earlier = (holder[:, None] == holder[None, :]) & (row_ids[None, :] < row_ids[:, None])
    order_rank = jnp.sum(earlier.astype(jnp.int32), axis=1)
    bucket_slot = jnp.where(visual, holder * capacity + order_rank, -1)
    placer = jnp.arange(holders * capacity, dtype=jnp.int32)[:, None] == bucket_slot[None, :]
    bucket_rows = jnp.dot(
        placer.astype(jnp.bfloat16), cot_flat, preferred_element_type=jnp.float32
    ).astype(jnp.bfloat16)
    bucket_ids = jnp.sum(jnp.where(placer, source[None, :] + 1, 0), axis=1) - 1
    arrived_rows, arrived_ids = (
        lax.all_to_all(bucket_rows, ("grp", "seq"), split_axis=0, concat_axis=0, tiled=True),
        lax.all_to_all(bucket_ids, ("grp", "seq"), split_axis=0, concat_axis=0, tiled=True),
    )
    local_index = arrived_ids - place * merged_rows
    setter = (jnp.arange(merged_rows, dtype=jnp.int32)[:, None] == local_index[None, :]).astype(
        jnp.bfloat16
    )
    returned = jnp.dot(setter, arrived_rows, preferred_element_type=jnp.float32)
    level_grads = jnp.transpose(returned.reshape(merged_rows, 2, cotangent.shape[2]), (1, 0, 2))
    return (merged, context, level_grads)


def solution(mesh):
    in_specs = (
        P(("grp", "seq"), "head"),
        P(),
        P(None, None, "head"),
        P("head", None),
        P(),
        P(None, ("grp", "seq"), "head"),
        P(("grp", "seq"), "head"),
        P(("grp", "seq")),
        P(("grp", "seq"), "head"),
        P(("grp", "seq"), "head"),
        P(("grp", "seq"), None, "head"),
    )
    out_specs = (
        P(None, ("grp", "seq"), "head"),
        P(("grp", "seq"), "head"),
        P(None, ("grp", "seq"), "head"),
    )
    return jax.shard_map(shards, mesh=mesh, in_specs=in_specs, out_specs=out_specs, check_vma=False)
```

profile of v0, /device:TPU:1, one launch (start us, length us, event | category | flops | bytes accessed | tf_op | source)
XLA Modules:
  0.0 407.7 jit_solution(7405874651068068960)
XLA Ops:
  7.2 0.7 all-gather.6.cloned.1.call-update
  7.9 1.5 broadcast_in_dim.55
  9.4 7.5 %all-to-all-start = ((bf16[8,128,144]{1,2,0:T(8,128)(2,1)}), bf16[8,128,144]{1,2,0:T(8,128)(2,1)S(1)}, u32[]{:S(2)}, u32[]{:S(2)}) async-start(bf16[8,128,144]{1,2,0:T(8,128)(2,1)} %broadcast_in_dim.55), calls=%async_computation | async-start | bytes 589824 | tf_op jit(solution)/shard_map/all_to_all | solution.py:19
  16.9 0.8 pad_dynamic-slice_fusion
  17.7 0.8 dynamic_slice.6
  18.4 0.1 broadcast_compare_fusion
  18.6 6.1 %all-to-all-done = bf16[8,128,144]{1,2,0:T(8,128)(2,1)S(1)} async-done(((bf16[8,128,144]{1,2,0:T(8,128)(2,1)}), bf16[8,128,144]{1,2,0:T(8,128)(2,1)S(1)}, u32[]{:S(2)}, u32[]{:S(2)}) %all-to-all-start) | async-done | bytes 294944 | tf_op jit(solution)/shard_map/all_to_all | solution.py:19
  24.6 1.2 convolution_convert_fusion.5
  25.9 1.2 convolution_convert_fusion.4
  27.1 9.7 %collective-permute-start.1 = (bf16[128,288]{0,1:T(8,128)(2,1)S(1)}, bf16[128,288]{0,1:T(8,128)(2,1)S(1)}, u32[]{:S(2)}, u32[]{:S(2)}) collective-permute-start(bf16[128,288]{0,1:T(8,128)(2,1)S(1)} %pad_maximum_fusion.4), channel_id=1, source_target_pairs={{8,0},{16,8},{24,16},{32,24},{40,32},{48,40},{56,48},{64,56},{72,6... | collective-permute-start | bytes 221192 | tf_op jit(solution)/shard_map/ppermute | solution.py:37
  36.8 1.9 collective-permute-start
  38.7 1.2 convolution_convert_fusion.3
  40.0 4.7 %collective-permute-done = bf16[128,288]{0,1:T(8,128)(2,1)S(1)} collective-permute-done((bf16[128,288]{0,1:T(8,128)(2,1)S(1)}, bf16[128,288]{0,1:T(8,128)(2,1)S(1)}, u32[]{:S(2)}, u32[]{:S(2)}) %collective-permute-start) | collective-permute-done | bytes 73760 | tf_op jit(solution)/shard_map/ppermute | solution.py:36
  44.7 0.4 fusion.79
  45.2 0.3 fusion.27
  45.4 0.3 fusion.39
  45.8 0.3 convolution_convert_fusion.1
  46.1 0.2 copy.44
  46.3 14.1 %all_to_all.38 = bf16[8,128,144]{1,2,0:T(8,128)(2,1)S(1)} all-to-all(bf16[8,128,144]{1,2,0:T(8,128)(2,1)S(1)} %bitcast.127), channel_id=1, replica_groups=mesh['grp'=2,'seq'=16,'head'=8] {'head'}, dimensions={0} | all-to-all | bytes 589824 | tf_op jit(solution)/shard_map/all_to_all | solution.py:55
  60.5 0.7 broadcast_in_dim.100
  61.2 3.4 all-to-all-start.2
  64.7 0.0 all-gather.12.cloned.1.call-start
  64.7 0.4 copy.43
  65.1 0.7 stack_reshape_reshape.6
  65.8 8.8 %all-to-all-done.2 = bf16[8,128,144]{1,2,0:T(8,128)(2,1)S(1)} async-done(((bf16[8,128,144]{1,2,0:T(8,128)(2,1)}), bf16[8,128,144]{1,2,0:T(8,128)(2,1)S(1)}, u32[]{:S(2)}, u32[]{:S(2)}) %all-to-all-start.2) | async-done | bytes 294944 | tf_op jit(solution)/shard_map/all_to_all | solution.py:19
  74.5 0.4 copy.45
  75.0 0.7 stack_reshape_reshape.7
  75.6 0.2 fusion.29
  75.9 21.8 %all-gather.6.cloned.1.call-done = bf16[2,4608,640]{2,1,0:T(8,128)(2,1)} async-done(((bf16[2,144,640]{2,1,0:T(8,128)(2,1)}), bf16[2,4608,640]{2,1,0:T(8,128)(2,1)}) %all-gather.6.cloned.1.call-update) | async-done | bytes 11796496 | tf_op jit(solution)/shard_map/all_gather | solution.py:143
  97.6 6.5 %convolution_convert_fusion.2 = bf16[2,32,640]{2,1,0:T(8,128)(2,1)S(1)} fusion(bf16[2,4608,640]{2,1,0:T(8,128)(2,1)} %all-gather.6.cloned.1.call-done, f32[2,4608]{1,0:T(2,128)S(1)} %copy-done.4, f32[2,32]{1,0:T(2,128)S(1)} %add_rsqrt_fusion, bf16[1,32,4608]{2,1,0:T(8,128)(2,1)S(1)} %stack_reshape_reshape.7, bf16[1,32,4608]{2,1,0:T(8,128)(2,1)S(1)} %stack_reshape_reshape.6), kind=kOutput, calls=%fused_computation.37 | convolution fusion | flops 379002880 | bytes 12505344 | tf_op jit(solution)/shard_map/lrk,lkc->lrc/dot_general | solution.py:140
  104.1 0.6 slice.34
  104.8 0.0 all-gather.8.cloned.1.call-start
  104.9 0.7 pad_maximum_fusion.2
  105.6 63.2 %all-gather.12.cloned.1.call-done = bf16[1,1024,640]{2,1,0:T(8,128)(2,1)} async-done(((bf16[1,32,640]{2,1,0:T(8,128)(2,1)}), bf16[1,1024,640]{2,1,0:T(8,128)(2,1)}) %all-gather.12.cloned.1.call-update) | async-done | bytes 1310736 | tf_op jit(solution)/shard_map/all_gather | solution.py:147
  168.8 1.9 fusion.20
  170.7 0.2 copy.46
  170.9 1.7 broadcast_in_dim.102
  172.6 6.1 %all-to-all-start.3 = ((bf16[8,256,640]{1,2,0:T(8,128)(2,1)}), bf16[8,256,640]{1,2,0:T(8,128)(2,1)S(1)}, u32[]{:S(2)}, u32[]{:S(2)}) async-start(bf16[8,256,640]{1,2,0:T(8,128)(2,1)} %broadcast_in_dim.102), calls=%async_computation.3 | async-start | bytes 5242880 | tf_op jit(solution)/shard_map/all_to_all | solution.py:19
  178.8 75.4 %all-gather.8.cloned.1.call-done = bf16[5120,768]{1,0:T(8,128)(2,1)} async-done(((bf16[160,768]{1,0:T(8,128)(2,1)}), bf16[5120,768]{1,0:T(8,128)(2,1)}) %all-gather.8.cloned.1.call-update) | async-done | bytes 7864336 | tf_op jit(solution)/shard_map/all_gather | solution.py:65
  254.2 4.2 %fusion.35 = bf16[256,256]{1,0:T(8,128)(2,1)} fusion(bf16[256,5120]{0,1:T(8,128)(2,1)S(1)} %bitcast.118, bf16[5120,768]{1,0:T(8,128)(2,1)} %all-gather.8.cloned.1.call-done), kind=kOutput, calls=%fused_computation.35 | convolution fusion | flops 671154176 | bytes 5373952 | tf_op jit(solution)/shard_map/dot_general | solution.py:159
  258.5 0.2 convert_reduce_fusion.1
  258.7 0.1 select_reduce_fusion
  258.8 0.7 sub.47
  259.5 6.4 %all-to-all-start.4 = ((s32[32,4,1]{1,2,0:T(1,128)}), s32[32,4,1]{1,2,0:T(1,128)S(1)}, u32[]{:S(2)}, u32[]{:S(2)}) async-start(s32[32,4,1]{1,2,0:T(1,128)} %bitcast.29), calls=%async_computation.4 | async-start | bytes 32768 | tf_op jit(solution)/shard_map/all_to_all | solution.py:201
  266.0 1.2 copy.58
  267.1 0.3 convolution_convert_fusion
  267.4 0.8 all_to_all.29
  268.2 5.5 %all-to-all-done.4 = s32[32,4,1]{1,2,0:T(1,128)S(1)} async-done(((s32[32,4,1]{1,2,0:T(1,128)}), s32[32,4,1]{1,2,0:T(1,128)S(1)}, u32[]{:S(2)}, u32[]{:S(2)}) %all-to-all-start.4) | async-done | bytes 544 | tf_op jit(solution)/shard_map/all_to_all | solution.py:201
  273.7 4.4 %all-to-all-start.5 = ((bf16[32,4,1280]{2,1,0:T(4,128)(2,1)}), bf16[32,4,1280]{2,1,0:T(4,128)(2,1)S(1)}, u32[]{:S(2)}, u32[]{:S(2)}) async-start(bf16[32,4,1280]{2,1,0:T(4,128)(2,1)} %all_to_all.29), calls=%async_computation.5 | async-start | bytes 655360 | tf_op jit(solution)/shard_map/all_to_all | solution.py:200
  278.1 1.4 iota_compare_fusion
  279.6 0.1 sub.50
  279.7 14.1 %all-to-all-done.5 = bf16[32,4,1280]{2,1,0:T(4,128)(2,1)S(1)} async-done(((bf16[32,4,1280]{2,1,0:T(4,128)(2,1)}), bf16[32,4,1280]{2,1,0:T(4,128)(2,1)S(1)}, u32[]{:S(2)}, u32[]{:S(2)}) %all-to-all-start.5) | async-done | bytes 327712 | tf_op jit(solution)/shard_map/all_to_all | solution.py:200
  293.8 0.1 all_to_all.31
  293.9 0.2 copy.52
  294.1 0.9 convolution_bitcast_fusion
  295.0 4.9 %fusion.32 = bf16[32,4,8,128]{3,2,1,0:T(8,128)(2,1)S(1)} fusion(bf16[256,5120]{0,1:T(8,128)(2,1)} %bitcast.119, bf16[5120,768]{1,0:T(8,128)(2,1)} %all-gather.8.cloned.1.call-done), kind=kOutput, calls=%fused_computation.34 | convolution fusion | flops 1342308352 | bytes 8126464 | tf_op jit(solution)/shard_map/dot_general | solution.py:158
  299.9 28.8 %all-gather.10.cloned.1.call-done = bf16[8192,256]{1,0:T(8,128)(2,1)} async-done(((bf16[256,256]{1,0:T(8,128)(2,1)}), bf16[8192,256]{1,0:T(8,128)(2,1)}) %all-gather.10.cloned.1.call-update) | async-done | bytes 4194320 | tf_op jit(solution)/shard_map/all_gather | solution.py:167
  328.7 6.9 %reshape.176 = bf16[8192,1,2,128]{3,2,0,1:T(2,128)(2,1)} reshape(bf16[8192,256]{1,0:T(8,128)(2,1)} %all-gather.10.cloned.1.call-done) | data formatting | bytes 8388608 | tf_op jit(solution)/shard_map/reshape | solution.py:170
  335.6 10.0 %fusion.77 = (bf16[8192,1,1,128]{3,2,0,1:T(2,128)(2,1)}, bf16[8192,1,1,128]{3,2,0,1:T(2,128)(2,1)}) fusion(bf16[8192,1,2,128]{3,2,0,1:T(2,128)(2,1)} %reshape.176), kind=kLoop, calls=%fused_computation.97 | loop fusion | bytes 8388608 | tf_op jit(solution)/shard_map/slice | solution.py:172
  345.6 9.2 %copy.55 = bf16[8192,1,1,128]{0,3,2,1:T(8,128)(2,1)} copy(bf16[8192,1,1,128]{3,2,0,1:T(2,128)(2,1)} %get-tuple-element.15) | data formatting | bytes 4194304
  354.8 15.5 %fusion.1 = (f32[4,256]{1,0:T(4,128)S(1)}, f32[8192,256,4]{1,0,2:T(8,128)}) fusion(pred[256,8192]{0,1:T(8,128)(4,1)S(1)} %iota_compare_fusion, bf16[32,4,8,128]{3,2,1,0:T(8,128)(2,1)S(1)} %fusion.32, bf16[8192,1,1,128]{3,2,0,1:T(2,128)(2,1)} %get-tuple-element.16), kind=kOutput, calls=%fused_computation.3 | convolution fusion | flops 2172648448 | bytes 38014976 | tf_op jit(solution)/shard_map/qhgd,khd->hgqk/dot_general | solution.py:173
  370.3 15.0 %fusion.2 = f32[4,256]{1,0:T(4,128)S(1)} fusion(f32[8192,256,4]{1,0,2:T(8,128)} %get-tuple-element.22, f32[4,256]{1,0:T(4,128)S(1)} %broadcast_maximum_fusion, pred[256,8192]{0,1:T(8,128)(4,1)S(1)} %iota_compare_fusion), kind=kLoop, calls=%fused_computation.4 | loop fusion | flops 41942016 | bytes 35659776 | tf_op jit(solution)/shard_map/reduce_sum | solution.py:179
  385.4 15.0 %fusion.45 = bf16[4,256,128]{1,2,0:T(8,128)(2,1)S(1)} fusion(f32[8192,256,4]{1,0,2:T(8,128)} %get-tuple-element.22, f32[4,256]{1,0:T(4,128)S(1)} %broadcast_maximum_fusion, pred[256,8192]{0,1:T(8,128)(4,1)S(1)} %iota_compare_fusion, bf16[8192,1,1,128]{0,3,2,1:T(8,128)(2,1)} %copy.55, f32[4,256]{1,0:T(4,128)S(1)} %fusion.2), kind=kOutput, calls=%fused_computation.46 | convolution fusion | flops 2189688832 | bytes 38019072 | tf_op jit(solution)/shard_map/hgqk,khd->hgqd/dot_general | solution.py:180
  400.4 0.8 copy.53
  (39 shorter events, 0.4 us)
Async XLA Ops:
  7.2 38.6 %copy-start = (bf16[144,1152]{1,0:T(8,128)(2,1)S(1)}, bf16[144,1152]{1,0:T(8,128)(2,1)}, u32[]{:S(2)}) copy-start(bf16[144,1152]{1,0:T(8,128)(2,1)} %param.14) | copy-start | bytes 995332
  7.2 53.3 %copy-start.6 = (bf16[128,144]{0,1:T(8,128)(2,1)S(1)}, bf16[128,144]{0,1:T(8,128)(2,1)}, u32[]{:S(2)}) copy-start(bf16[128,144]{0,1:T(8,128)(2,1)} %param.11) | copy-start | bytes 110596
  7.2 90.4 %all-gather.6.cloned.1.call-start = ((), (), s32[]{:S(2)}) async-start(), calls=%async_computation.6 | async-start | bytes 12165120 | tf_op jit(solution)/shard_map/all_gather | solution.py:143
  9.4 15.2 %all-to-all-start = ((bf16[8,128,144]{1,2,0:T(8,128)(2,1)}), bf16[8,128,144]{1,2,0:T(8,128)(2,1)S(1)}, u32[]{:S(2)}, u32[]{:S(2)}) async-start(bf16[8,128,144]{1,2,0:T(8,128)(2,1)} %broadcast_in_dim.55), calls=%async_computation | async-start | bytes 589824 | tf_op jit(solution)/shard_map/all_to_all | solution.py:19
  27.1 12.9 %collective-permute-start.1 = (bf16[128,288]{0,1:T(8,128)(2,1)S(1)}, bf16[128,288]{0,1:T(8,128)(2,1)S(1)}, u32[]{:S(2)}, u32[]{:S(2)}) collective-permute-start(bf16[128,288]{0,1:T(8,128)(2,1)S(1)} %pad_maximum_fusion.4), channel_id=1, source_target_pairs={{8,0},{16,8},{24,16},{32,24},{40,32},{48,40},{56,48},{64,56},{72,6... | collective-permute-start | bytes 221192 | tf_op jit(solution)/shard_map/ppermute | solution.py:37
  36.8 7.9 %collective-permute-start = (bf16[128,288]{0,1:T(8,128)(2,1)S(1)}, bf16[128,288]{0,1:T(8,128)(2,1)S(1)}, u32[]{:S(2)}, u32[]{:S(2)}) collective-permute-start(bf16[128,288]{0,1:T(8,128)(2,1)S(1)} %pad_maximum_fusion.4), channel_id=1, source_target_pairs={{0,8},{8,16},{16,24},{24,32},{32,40},{40,48},{48,56},{56,64},{64,7... | collective-permute-start | bytes 221192 | tf_op jit(solution)/shard_map/ppermute | solution.py:36
  40.0 57.7 %copy-start.4 = (f32[2,4608]{1,0:T(2,128)S(1)}, f32[2,4608]{1,0:T(2,128)}, u32[]{:S(2)}) copy-start(f32[2,4608]{1,0:T(2,128)} %param.15) | copy-start | bytes 110596
  61.2 13.3 %all-to-all-start.2 = ((bf16[8,128,144]{1,2,0:T(8,128)(2,1)}), bf16[8,128,144]{1,2,0:T(8,128)(2,1)S(1)}, u32[]{:S(2)}, u32[]{:S(2)}) async-start(bf16[8,128,144]{1,2,0:T(8,128)(2,1)} %broadcast_in_dim.100), calls=%async_computation.2 | async-start | bytes 589824 | tf_op jit(solution)/shard_map/all_to_all | solution.py:19
  64.7 104.1 %all-gather.12.cloned.1.call-start = ((), (), s32[]{:S(2)}) async-start(), calls=%async_computation.9 | async-start | bytes 1351680 | tf_op jit(solution)/shard_map/all_gather | solution.py:147
  75.8 29.0 %copy-start.5 = (bf16[160,512]{1,0:T(8,128)(2,1)S(1)}, bf16[160,512]{1,0:T(8,128)(2,1)}, u32[]{:S(2)}) copy-start(bf16[160,512]{1,0:T(8,128)(2,1)} %param.19) | copy-start | bytes 491524
  75.8 29.0 %copy-start.7 = (bf16[160,256]{1,0:T(8,128)(2,1)S(1)}, bf16[160,256]{1,0:T(8,128)(2,1)}, u32[]{:S(2)}) copy-start(bf16[160,256]{1,0:T(8,128)(2,1)} %param.20) | copy-start | bytes 245764
  75.8 92.9 %copy-start.8 = (s32[256]{0:T(256)S(1)}, s32[256]{0:T(256)}, u32[]{:S(2)}) copy-start(s32[256]{0:T(256)} %param.18) | copy-start | bytes 3076
  75.9 92.9 %copy-start.9 = (bf16[256,640]{1,0:T(8,128)(2,1)S(1)}, bf16[256,640]{1,0:T(8,128)(2,1)}, u32[]{:S(2)}) copy-start(bf16[256,640]{1,0:T(8,128)(2,1)} %param.17) | copy-start | bytes 983044
  104.1 68.5 %copy-start.3 = (bf16[2,32,640]{2,1,0:T(8,128)(2,1)}, bf16[2,32,640]{2,1,0:T(8,128)(2,1)S(1)}, u32[]{:S(2)}) copy-start(bf16[2,32,640]{2,1,0:T(8,128)(2,1)S(1)} %convolution_convert_fusion.2) | copy-start | bytes 245764
  104.8 149.4 %all-gather.8.cloned.1.call-start = ((), (), s32[]{:S(2)}) async-start(), calls=%async_computation.7 | async-start | bytes 8110080 | tf_op jit(solution)/shard_map/all_gather | solution.py:65
  172.6 81.6 %all-to-all-start.3 = ((bf16[8,256,640]{1,2,0:T(8,128)(2,1)}), bf16[8,256,640]{1,2,0:T(8,128)(2,1)S(1)}, u32[]{:S(2)}, u32[]{:S(2)}) async-start(bf16[8,256,640]{1,2,0:T(8,128)(2,1)} %broadcast_in_dim.102), calls=%async_computation.3 | async-start | bytes 5242880 | tf_op jit(solution)/shard_map/all_to_all | solution.py:19
  178.8 149.9 %all-gather.10.cloned.1.call-start = ((), (), s32[]{:S(2)}) async-start(), calls=%async_computation.8 | async-start | bytes 4325376 | tf_op jit(solution)/shard_map/all_gather | solution.py:167
  254.2 13.2 %copy-start.2 = (bf16[8,256,640]{1,2,0:T(8,128)(2,1)}, bf16[8,256,640]{1,2,0:T(8,128)(2,1)S(1)}, u32[]{:S(2)}) copy-start(bf16[8,256,640]{1,2,0:T(8,128)(2,1)S(1)} %all-to-all-done.3) | copy-start | bytes 7864324
  259.5 14.2 %all-to-all-start.4 = ((s32[32,4,1]{1,2,0:T(1,128)}), s32[32,4,1]{1,2,0:T(1,128)S(1)}, u32[]{:S(2)}, u32[]{:S(2)}) async-start(s32[32,4,1]{1,2,0:T(1,128)} %bitcast.29), calls=%async_computation.4 | async-start | bytes 32768 | tf_op jit(solution)/shard_map/all_to_all | solution.py:201
  273.7 20.1 %all-to-all-start.5 = ((bf16[32,4,1280]{2,1,0:T(4,128)(2,1)}), bf16[32,4,1280]{2,1,0:T(4,128)(2,1)S(1)}, u32[]{:S(2)}, u32[]{:S(2)}) async-start(bf16[32,4,1280]{2,1,0:T(4,128)(2,1)} %all_to_all.29), calls=%async_computation.5 | async-start | bytes 655360 | tf_op jit(solution)/shard_map/all_to_all | solution.py:200
  385.3 15.9 %copy-start.1 = (bf16[144,1152]{1,0:T(8,128)(2,1)S(1)}, bf16[144,1152]{1,0:T(8,128)(2,1)}, u32[]{:S(2)}) copy-start(bf16[144,1152]{1,0:T(8,128)(2,1)} %param.14) | copy-start | bytes 995332
Sparse Core Ops, SparseCore 0:
  9.9 87.7 all-gather.5
  104.9 63.8 all-gather.11
  171.2 82.9 all-gather.7
  258.6 70.0 all-gather.9
where the time goes:
time: 409 us; the launch traced here: 408 us
  waiting for transfers between devices  229 us (56%)
  matrix products  54.2 us (13%)
  starting transfers between devices  39.5 us (10%)
  local copies, waits for them, and re-layouts  38.8 us (9%)
  other arithmetic  17.9 us (4%)
  blocking collectives  14.1 us (3%)
  between operations  14.1 us (3%)
    all_gather x1, waiting for transfers between devices, in_one_piece(): lax.all_gather(both, axis, axis=dim, tiled=True)  75.4 us
    all_gather x1, waiting for transfers between devices, shards(): piece = lax.all_gather(merged[0], ('grp', 'seq'), axis=0, tiled=True)  63.2 us
    all_gather x1, waiting for transfers between devices, shards(): piece = lax.all_gather(keys_values, ('grp', 'seq'), axis=0, tiled=True)  28.8 us
    all_gather x1, waiting for transfers between devices, shards(): lax.all_gather(merge_w, ('grp', 'seq'), axis=1, tiled=True)  21.8 us
    all_to_all x3, starting transfers between devices, from_everyone(): lax.all_to_all(jnp.broadcast_to(value[None], (length, *value.shape)), axi...  17 us
    dot_general x1, matrix products, shards(): jnp.einsum('qhgd,khd->hgqk', query4, keys, preferred_element_type=jnp.flo...  15.5 us
    reduce_sum x1, other arithmetic, shards(): new_sum = jnp.sum(probs, axis=3)  15 us
    dot_general x1, matrix products, shards(): jnp.einsum('hgqk,khd->hgqd', probs.astype(jnp.bfloat16), values, preferre...  15 us
  transfers between devices with their start and end apart: 11, of which 9 were waited for; matrix products, arithmetic and copies ran while one was open for 6% of the time, Pallas kernels for 0%

commit v1 on v0

--- a/solution.py
+++ b/solution.py
@@ -140,7 +140,12 @@
     merged = jnp.einsum(
         "lrk,lkc->lrc",
         block,
-        lax.all_gather(merge_w, ("grp", "seq"), axis=1, tiled=True),
+        jnp.concatenate(
+            lax.all_to_all(
+                jnp.stack([merge_w] * lax.axis_size(("grp", "seq"))), ("grp", "seq"), 0, 0
+            ),
+            axis=1,
+        ),
         preferred_element_type=jnp.float32,
     ).astype(jnp.bfloat16)
     tok_rows = embedded.shape[0]

time: 409 us -> 659 us (1.61)
  waiting for transfers between devices: 229 us -> 462 us
  local copies, waits for them, and re-layouts: 38.8 us -> 49.2 us
  blocking collectives: 14.1 us -> 21.4 us
    all_to_all x0 -> x1, waiting for transfers between devices: none -> 255 us  [shards(): lax.all_to_all(jnp.stack([merge_w] * lax.axis_size(('grp', 'seq'))), ('gr...]
    all_gather x1 -> x0, waiting for transfers between devices: 21.8 us -> none  [shards(): lax.all_gather(merge_w, ('grp', 'seq'), axis=1, tiled=True)]
    all_to_all x0 -> x1, blocking collectives: none -> 10.4 us  [from_everyone(): lax.all_to_all(jnp.broadcast_to(value[None], (length, *value.shape)), axi...]
    all_gather x1, waiting for transfers between devices: 63.2 us -> 72.3 us  [shards(): piece = lax.all_gather(merged[0], ('grp', 'seq'), axis=0, tiled=True)]
    all_to_all x3 -> x2, waiting for transfers between devices: 14.9 us -> 6.07 us  [from_everyone(): lax.all_to_all(jnp.broadcast_to(value[None], (length, *value.shape)), axi...]
    all_to_all x3 -> x2, starting transfers between devices: 17 us -> 13.6 us  [from_everyone(): lax.all_to_all(jnp.broadcast_to(value[None], (length, *value.shape)), axi...]
  transfers between devices with their start and end apart: 11 -> 10, of which waited for: 9 -> 8; matrix products, arithmetic and copies ran while one was open for 6% -> 3% of each run, Pallas kernels for 0% -> 0%
where the time goes in v1:
time: 659 us; the launch traced here: 657 us
  waiting for transfers between devices  462 us (70%)
  matrix products  49.9 us (8%)
  local copies, waits for them, and re-layouts  49.2 us (7%)
  starting transfers between devices  42.6 us (6%)
  blocking collectives  21.4 us (3%)
  other arithmetic  17.9 us (3%)
  between operations  14.1 us (2%)
    all_to_all x1, waiting for transfers between devices, shards(): lax.all_to_all(jnp.stack([merge_w] * lax.axis_size(('grp', 'seq'))), ('gr...  255 us
    all_gather x1, waiting for transfers between devices, in_one_piece(): lax.all_gather(both, axis, axis=dim, tiled=True)  75.4 us
    all_gather x1, waiting for transfers between devices, shards(): piece = lax.all_gather(merged[0], ('grp', 'seq'), axis=0, tiled=True)  72.3 us
    all_gather x1, waiting for transfers between devices, shards(): piece = lax.all_gather(keys_values, ('grp', 'seq'), axis=0, tiled=True)  29 us
    dot_general x1, matrix products, shards(): jnp.einsum('qhgd,khd->hgqk', query4, keys, preferred_element_type=jnp.flo...  15.5 us
    reduce_sum x1, other arithmetic, shards(): new_sum = jnp.sum(probs, axis=3)  15 us
    dot_general x1, matrix products, shards(): jnp.einsum('hgqk,khd->hgqd', probs.astype(jnp.bfloat16), values, preferre...  15 us
    all_to_all x1, waiting for transfers between devices, shards(): lax.all_to_all(bucket_rows, ('grp', 'seq'), split_axis=0, concat_axis=0,...  14.1 us
  transfers between devices with their start and end apart: 10, of which 8 were waited for; matrix products, arithmetic and copies ran while one was open for 3% of the time, Pallas kernels for 0%

profile of v1, /device:TPU:1, one launch (start us, length us, event | category | flops | bytes accessed | tf_op | source)
XLA Modules:
  0.0 657.1 jit_solution(6125903520941959538)
XLA Ops:
  7.2 1.6 broadcast_in_dim.55
  8.8 7.5 %all-to-all-start = ((bf16[8,128,144]{1,2,0:T(8,128)(2,1)}), bf16[8,128,144]{1,2,0:T(8,128)(2,1)S(1)}, u32[]{:S(2)}, u32[]{:S(2)}) async-start(bf16[8,128,144]{1,2,0:T(8,128)(2,1)} %broadcast_in_dim.55), calls=%async_computation | async-start | bytes 589824 | tf_op jit(solution)/shard_map/all_to_all | solution.py:19
  16.2 0.8 pad_dynamic-slice_fusion
  17.0 0.8 dynamic_slice.6
  17.8 0.1 broadcast_compare_fusion
  17.9 6.1 all-to-all-done
  24.0 1.2 convolution_convert_fusion.5
  25.2 1.2 convolution_convert_fusion.4
  26.4 9.7 %collective-permute-start.1 = (bf16[128,288]{0,1:T(8,128)(2,1)S(1)}, bf16[128,288]{0,1:T(8,128)(2,1)S(1)}, u32[]{:S(2)}, u32[]{:S(2)}) collective-permute-start(bf16[128,288]{0,1:T(8,128)(2,1)S(1)} %pad_maximum_fusion.4), channel_id=1, source_target_pairs={{8,0},{16,8},{24,16},{32,24},{40,32},{48,40},{56,48},{64,56},{72,6... | collective-permute-start | bytes 221192 | tf_op jit(solution)/shard_map/ppermute | solution.py:37
  36.1 1.9 collective-permute-start
  38.1 1.2 convolution_convert_fusion.3
  39.3 4.6 collective-permute-done
  44.0 0.4 fusion.79
  44.4 0.3 fusion.27
  44.7 0.3 fusion.39
  45.0 0.3 convolution_convert_fusion.1
  45.3 0.2 copy.45
  45.5 11.0 %all_to_all.43 = bf16[8,128,144]{1,2,0:T(8,128)(2,1)S(1)} all-to-all(bf16[8,128,144]{1,2,0:T(8,128)(2,1)S(1)} %bitcast.130), channel_id=1, replica_groups=mesh['grp'=2,'seq'=16,'head'=8] {'head'}, dimensions={0} | all-to-all | bytes 589824 | tf_op jit(solution)/shard_map/all_to_all | solution.py:55
  56.6 10.4 %all_to_all.44 = bf16[8,128,144]{1,2,0:T(8,128)(2,1)S(1)} all-to-all(bf16[8,128,144]{1,2,0:T(8,128)(2,1)S(1)} %broadcast_in_dim.100), channel_id=1, replica_groups=mesh['grp'=2,'seq'=16,'head'=8] {'head'}, dimensions={0} | all-to-all | bytes 589824 | tf_op jit(solution)/shard_map/all_to_all | solution.py:19
  67.0 5.2 stack.5
  72.2 6.5 all-to-all-start.3
  78.7 0.0 all-gather.9.cloned.1.call-start
  78.7 0.4 copy.44
  79.1 0.7 stack_reshape_reshape.6
  79.8 0.4 copy.46
  80.2 0.7 stack_reshape_reshape.7
  80.9 0.2 fusion.29
  81.1 255.0 %all-to-all-done.3 = bf16[32,2,144,640]{3,2,1,0:T(8,128)(2,1)} async-done(((bf16[32,2,144,640]{3,2,1,0:T(8,128)(2,1)}), bf16[32,2,144,640]{3,2,1,0:T(8,128)(2,1)}, u32[]{:S(2)}, u32[]{:S(2)}) %all-to-all-start.3) | async-done | bytes 11796512 | tf_op jit(solution)/shard_map/all_to_all | solution.py:144
  336.1 6.0 copy.47
  342.2 2.1 convolution_convert_fusion.2
  344.4 0.6 slice.34
  345.0 0.0 all-gather.5.cloned.1.call-start
  345.1 0.7 pad_maximum_fusion.2
  345.8 72.3 %all-gather.9.cloned.1.call-done = bf16[1,1024,640]{2,1,0:T(8,128)(2,1)} async-done(((bf16[1,32,640]{2,1,0:T(8,128)(2,1)}), bf16[1,1024,640]{2,1,0:T(8,128)(2,1)}) %all-gather.9.cloned.1.call-update) | async-done | bytes 1310736 | tf_op jit(solution)/shard_map/all_gather | solution.py:152
  418.1 1.9 fusion.20
  420.0 0.2 copy.48
  420.2 1.7 broadcast_in_dim.102
  422.0 6.1 all-to-all-start.4
  428.1 75.4 %all-gather.5.cloned.1.call-done = bf16[5120,768]{1,0:T(8,128)(2,1)} async-done(((bf16[160,768]{1,0:T(8,128)(2,1)}), bf16[5120,768]{1,0:T(8,128)(2,1)}) %all-gather.5.cloned.1.call-update) | async-done | bytes 7864336 | tf_op jit(solution)/shard_map/all_gather | solution.py:65
  503.5 4.2 fusion.35
  507.8 0.2 convert_reduce_fusion.1
  508.0 0.1 select_reduce_fusion
  508.1 0.7 sub.47
  508.8 6.4 all-to-all-start.5
  515.3 1.2 copy.60
  516.4 0.3 convolution_convert_fusion
  516.7 0.8 all_to_all.33
  517.5 5.5 all-to-all-done.5
  523.0 4.4 all-to-all-start.6
  527.4 1.4 iota_compare_fusion
  528.9 0.1 sub.50
  529.0 14.1 %all-to-all-done.6 = bf16[32,4,1280]{2,1,0:T(4,128)(2,1)S(1)} async-done(((bf16[32,4,1280]{2,1,0:T(4,128)(2,1)}), bf16[32,4,1280]{2,1,0:T(4,128)(2,1)S(1)}, u32[]{:S(2)}, u32[]{:S(2)}) %all-to-all-start.6) | async-done | bytes 327712 | tf_op jit(solution)/shard_map/all_to_all | solution.py:205
  543.1 0.1 all_to_all.35
  543.2 0.2 copy.54
  543.4 0.9 convolution_bitcast_fusion
  544.3 4.9 fusion.32
  549.2 29.0 %all-gather.7.cloned.1.call-done = bf16[8192,256]{1,0:T(8,128)(2,1)} async-done(((bf16[256,256]{1,0:T(8,128)(2,1)}), bf16[8192,256]{1,0:T(8,128)(2,1)}) %all-gather.7.cloned.1.call-update) | async-done | bytes 4194320 | tf_op jit(solution)/shard_map/all_gather | solution.py:172
  578.1 6.9 %reshape.186 = bf16[8192,1,2,128]{3,2,0,1:T(2,128)(2,1)} reshape(bf16[8192,256]{1,0:T(8,128)(2,1)} %all-gather.7.cloned.1.call-done) | data formatting | bytes 8388608 | tf_op jit(solution)/shard_map/reshape | solution.py:175
  585.0 9.9 %fusion.77 = (bf16[8192,1,1,128]{3,2,0,1:T(2,128)(2,1)}, bf16[8192,1,1,128]{3,2,0,1:T(2,128)(2,1)}) fusion(bf16[8192,1,2,128]{3,2,0,1:T(2,128)(2,1)} %reshape.186), kind=kLoop, calls=%fused_computation.97 | loop fusion | bytes 8388608 | tf_op jit(solution)/shard_map/slice | solution.py:177
  594.9 9.2 %copy.57 = bf16[8192,1,1,128]{0,3,2,1:T(8,128)(2,1)} copy(bf16[8192,1,1,128]{3,2,0,1:T(2,128)(2,1)} %get-tuple-element.15) | data formatting | bytes 4194304
  604.1 15.5 %fusion.1 = (f32[4,256]{1,0:T(4,128)S(1)}, f32[8192,256,4]{1,0,2:T(8,128)}) fusion(pred[256,8192]{0,1:T(8,128)(4,1)S(1)} %iota_compare_fusion, bf16[32,4,8,128]{3,2,1,0:T(8,128)(2,1)S(1)} %fusion.32, bf16[8192,1,1,128]{3,2,0,1:T(2,128)(2,1)} %get-tuple-element.16), kind=kOutput, calls=%fused_computation.3 | convolution fusion | flops 2172648448 | bytes 38014976 | tf_op jit(solution)/shard_map/qhgd,khd->hgqk/dot_general | solution.py:178
  619.6 15.0 %fusion.2 = f32[4,256]{1,0:T(4,128)S(1)} fusion(f32[8192,256,4]{1,0,2:T(8,128)} %get-tuple-element.22, f32[4,256]{1,0:T(4,128)S(1)} %broadcast_maximum_fusion, pred[256,8192]{0,1:T(8,128)(4,1)S(1)} %iota_compare_fusion), kind=kLoop, calls=%fused_computation.4 | loop fusion | flops 41942016 | bytes 35659776 | tf_op jit(solution)/shard_map/reduce_sum | solution.py:184
  634.7 15.0 %fusion.45 = bf16[4,256,128]{1,2,0:T(8,128)(2,1)S(1)} fusion(f32[8192,256,4]{1,0,2:T(8,128)} %get-tuple-element.22, f32[4,256]{1,0:T(4,128)S(1)} %broadcast_maximum_fusion, pred[256,8192]{0,1:T(8,128)(4,1)S(1)} %iota_compare_fusion, bf16[8192,1,1,128]{0,3,2,1:T(8,128)(2,1)} %copy.57, f32[4,256]{1,0:T(4,128)S(1)} %fusion.2), kind=kOutput, calls=%fused_computation.46 | convolution fusion | flops 2189688832 | bytes 38019072 | tf_op jit(solution)/shard_map/hgqk,khd->hgqd/dot_general | solution.py:185
  649.7 0.8 copy.55
  (41 shorter events, 0.4 us)
Async XLA Ops:
  7.2 37.8 %copy-start = (bf16[144,1152]{1,0:T(8,128)(2,1)S(1)}, bf16[144,1152]{1,0:T(8,128)(2,1)}, u32[]{:S(2)}) copy-start(bf16[144,1152]{1,0:T(8,128)(2,1)} %param.14) | copy-start | bytes 995332
  7.2 49.4 %copy-start.7 = (bf16[128,144]{0,1:T(8,128)(2,1)S(1)}, bf16[128,144]{0,1:T(8,128)(2,1)}, u32[]{:S(2)}) copy-start(bf16[128,144]{0,1:T(8,128)(2,1)} %param.11) | copy-start | bytes 110596
  7.2 59.8 %copy-start.5 = (bf16[2,144,640]{2,1,0:T(8,128)(2,1)S(1)}, bf16[2,144,640]{2,1,0:T(8,128)(2,1)}, u32[]{:S(2)}) copy-start(bf16[2,144,640]{2,1,0:T(8,128)(2,1)} %param.16) | copy-start | bytes 1105924
  8.8 15.2 %all-to-all-start = ((bf16[8,128,144]{1,2,0:T(8,128)(2,1)}), bf16[8,128,144]{1,2,0:T(8,128)(2,1)S(1)}, u32[]{:S(2)}, u32[]{:S(2)}) async-start(bf16[8,128,144]{1,2,0:T(8,128)(2,1)} %broadcast_in_dim.55), calls=%async_computation | async-start | bytes 589824 | tf_op jit(solution)/shard_map/all_to_all | solution.py:19
  26.4 12.9 %collective-permute-start.1 = (bf16[128,288]{0,1:T(8,128)(2,1)S(1)}, bf16[128,288]{0,1:T(8,128)(2,1)S(1)}, u32[]{:S(2)}, u32[]{:S(2)}) collective-permute-start(bf16[128,288]{0,1:T(8,128)(2,1)S(1)} %pad_maximum_fusion.4), channel_id=1, source_target_pairs={{8,0},{16,8},{24,16},{32,24},{40,32},{48,40},{56,48},{64,56},{72,6... | collective-permute-start | bytes 221192 | tf_op jit(solution)/shard_map/ppermute | solution.py:37
  36.1 7.8 %collective-permute-start = (bf16[128,288]{0,1:T(8,128)(2,1)S(1)}, bf16[128,288]{0,1:T(8,128)(2,1)S(1)}, u32[]{:S(2)}, u32[]{:S(2)}) collective-permute-start(bf16[128,288]{0,1:T(8,128)(2,1)S(1)} %pad_maximum_fusion.4), channel_id=1, source_target_pairs={{0,8},{8,16},{16,24},{24,32},{32,40},{40,48},{48,56},{56,64},{64,7... | collective-permute-start | bytes 221192 | tf_op jit(solution)/shard_map/ppermute | solution.py:36
  72.2 263.9 %all-to-all-start.3 = ((bf16[32,2,144,640]{3,2,1,0:T(8,128)(2,1)}), bf16[32,2,144,640]{3,2,1,0:T(8,128)(2,1)}, u32[]{:S(2)}, u32[]{:S(2)}) async-start(bf16[32,2,144,640]{3,2,1,0:T(8,128)(2,1)} %stack.5), calls=%async_computation.3 | async-start | bytes 23592960 | tf_op jit(solution)/shard_map/all_to_all | solution.py:144
  78.7 339.4 %all-gather.9.cloned.1.call-start = ((), (), s32[]{:S(2)}) async-start(), calls=%async_computation.9 | async-start | bytes 1351680 | tf_op jit(solution)/shard_map/all_gather | solution.py:152
  336.1 6.1 copy-start.4
  342.2 2.9 copy-start.6
  342.2 2.9 copy-start.8
  342.2 75.9 %copy-start.9 = (s32[256]{0:T(256)S(1)}, s32[256]{0:T(256)}, u32[]{:S(2)}) copy-start(s32[256]{0:T(256)} %param.18) | copy-start | bytes 3076
  342.2 75.9 %copy-start.10 = (bf16[256,640]{1,0:T(8,128)(2,1)S(1)}, bf16[256,640]{1,0:T(8,128)(2,1)}, u32[]{:S(2)}) copy-start(bf16[256,640]{1,0:T(8,128)(2,1)} %param.17) | copy-start | bytes 983044
  344.3 163.4 %copy-start.3 = (bf16[2,32,640]{2,1,0:T(8,128)(2,1)}, bf16[2,32,640]{2,1,0:T(8,128)(2,1)S(1)}, u32[]{:S(2)}) copy-start(bf16[2,32,640]{2,1,0:T(8,128)(2,1)S(1)} %convolution_convert_fusion.2) | copy-start | bytes 245764
  345.0 158.5 %all-gather.5.cloned.1.call-start = ((), (), s32[]{:S(2)}) async-start(), calls=%async_computation.7 | async-start | bytes 8110080 | tf_op jit(solution)/shard_map/all_gather | solution.py:65
  422.0 81.6 %all-to-all-start.4 = ((bf16[8,256,640]{1,2,0:T(8,128)(2,1)}), bf16[8,256,640]{1,2,0:T(8,128)(2,1)S(1)}, u32[]{:S(2)}, u32[]{:S(2)}) async-start(bf16[8,256,640]{1,2,0:T(8,128)(2,1)} %broadcast_in_dim.102), calls=%async_computation.4 | async-start | bytes 5242880 | tf_op jit(solution)/shard_map/all_to_all | solution.py:19
  428.1 150.1 %all-gather.7.cloned.1.call-start = ((), (), s32[]{:S(2)}) async-start(), calls=%async_computation.8 | async-start | bytes 4325376 | tf_op jit(solution)/shard_map/all_gather | solution.py:172
  503.5 19.5 %copy-start.2 = (bf16[8,256,640]{1,2,0:T(8,128)(2,1)}, bf16[8,256,640]{1,2,0:T(8,128)(2,1)S(1)}, u32[]{:S(2)}) copy-start(bf16[8,256,640]{1,2,0:T(8,128)(2,1)S(1)} %all-to-all-done.4) | copy-start | bytes 7864324
  508.8 14.2 %all-to-all-start.5 = ((s32[32,4,1]{1,2,0:T(1,128)}), s32[32,4,1]{1,2,0:T(1,128)S(1)}, u32[]{:S(2)}, u32[]{:S(2)}) async-start(s32[32,4,1]{1,2,0:T(1,128)} %bitcast.31), calls=%async_computation.5 | async-start | bytes 32768 | tf_op jit(solution)/shard_map/all_to_all | solution.py:206
  523.0 20.1 %all-to-all-start.6 = ((bf16[32,4,1280]{2,1,0:T(4,128)(2,1)}), bf16[32,4,1280]{2,1,0:T(4,128)(2,1)S(1)}, u32[]{:S(2)}, u32[]{:S(2)}) async-start(bf16[32,4,1280]{2,1,0:T(4,128)(2,1)} %all_to_all.33), calls=%async_computation.6 | async-start | bytes 655360 | tf_op jit(solution)/shard_map/all_to_all | solution.py:205
  634.7 15.9 %copy-start.1 = (bf16[144,1152]{1,0:T(8,128)(2,1)S(1)}, bf16[144,1152]{1,0:T(8,128)(2,1)}, u32[]{:S(2)}) copy-start(bf16[144,1152]{1,0:T(8,128)(2,1)} %param.14) | copy-start | bytes 995332
Sparse Core Ops, SparseCore 0:
  345.1 72.9 all-gather.8
  420.5 82.9 all-gather.4
  507.9 70.1 all-gather.6
